TPU v7x, 32 devices: a whole 2x2x4 slice. The times are simulated.
32 devices in a mesh: fsdp: 4 (over y, core), sp: 8 (over z, x).
Axes of the slice: x: 2, y: 2, z: 4, core: 2. Of those that a mesh axis runs over, the one named last changes fastest.
Arguments:
- hidden: bfloat16 [2048, 8192], P('sp', 'fsdp'), may hold values from -23 to 23
- w_query: bfloat16 [8192, 1024], P('fsdp', 'sp'), may hold values from -0.125 to 0.125
- w_keyvalue: bfloat16 [8192, 256], P('fsdp', 'sp'), may hold values from -0.125 to 0.125
- w_output: bfloat16 [1024, 8192], P('sp', 'fsdp'), may hold values from -0.75 to 0.75
- segment_ids: int32 [2048], P('sp'), may hold values from 0 to 7, never falling along the last dimension, each value on 1 to 512 neighbouring positions
Outputs:
- attended: bfloat16 [2048, 8192], P('sp', 'fsdp')
Inputs may be any that keep to these rules, and one draw needn't show every extreme that they name: `segment_ids`: segment ids never fall along the sequence; every episode has between 1 and 512 tokens.
All inputs are finite; a program needn't handle non-finite values.
Results may differ from a plain program's by a relative error of at most 0.0085.
The roundings to bfloat16 on the way count: a program that leaves them out, or rounds other values in their place, can miss the bound.
Values may be sent and summed in bfloat16 or wider, within the bound.
A program may use at most 128 MiB of HBM per device.

v0:
```python
import math
import jax
import jax.numpy as jnp
from jax import lax
from jax.sharding import PartitionSpec as P

HD = 128
GROUP = 8
ROPE_BASE = 500000.0
NEG_FILL = -1e30


def rotate(values, positions, head_count, width):
    row_count = values.shape[0]
    shaped = values.reshape(row_count, head_count, width)
    half_width = width // 2
    frequency = jnp.exp(
        jnp.arange(half_width, dtype=jnp.float32) * (-2.0 * math.log(ROPE_BASE) / width)
    )
    angles = positions.astype(jnp.float32)[:, None] * frequency[None, :]
    cosine = jnp.cos(angles)[:, None, :]
    sine_part = jnp.sin(angles)[:, None, :]
    lower_half = shaped[:, :, :half_width]
    upper_half = shaped[:, :, half_width:]
    turned = jnp.concatenate(
        [
            lower_half * cosine - upper_half * sine_part,
            upper_half * cosine + lower_half * sine_part,
        ],
        axis=2,
    )
    return turned.reshape(row_count, head_count * width)


def split_keys(kv_sum, positions, kv_count, width):
    row_count = kv_sum.shape[0]
    shaped = kv_sum.reshape(row_count, kv_count, 2, width)
    key_part = rotate(
        shaped[:, :, 0, :].reshape(row_count, kv_count * width), positions, kv_count, width
    )
    key_part = key_part.reshape(row_count, kv_count, 1, width)
    return jnp.concatenate([key_part, shaped[:, :, 1:2, :]], axis=2).astype(jnp.bfloat16)


def merge_keys(
    state_in, query_tile, query_pos_tile, query_seg_tile, key_tile, key_pos_tile, key_seg_tile
):
    running_max, running_sum, weighted = state_in
    allowed = (key_pos_tile[None, :] <= query_pos_tile[:, None]) & (
        key_seg_tile[None, :] == query_seg_tile[:, None]
    )
    key_part = key_tile[:, :HD]
    value_part = key_tile[:, HD:]
    scores = lax.dot_general(
        query_tile, key_part, (((1,), (1,)), ((), ())), preferred_element_type=jnp.float32
    ) * HD ** (-0.5)
    masked = jnp.where(allowed, scores, NEG_FILL)
    new_max = jnp.maximum(running_max, jnp.max(masked, axis=1))
    weights = jnp.where(allowed, jnp.exp(masked - new_max[:, None]), 0.0)
    new_sum = jnp.sum(weights, axis=1)
    new_weighted = jnp.dot(
        weights.astype(jnp.bfloat16), value_part, preferred_element_type=jnp.float32
    )
    return (new_max, new_sum, new_weighted)


def on_device(hidden, w_query, w_keyvalue, w_output, segment_ids):
    fsdp_count = lax.axis_size("fsdp")
    seq_count = lax.axis_size("sp")
    fsdp_index = lax.axis_index("fsdp")
    seq_index = lax.axis_index("sp")
    tok_rows = hidden.shape[0]
    sub_rows = tok_rows // fsdp_count
    kv_count = seq_count // GROUP
    query_rows = seq_count * sub_rows
    offsets = jnp.arange(query_rows, dtype=jnp.int32)
    query_pos = offsets // sub_rows * tok_rows + fsdp_index * sub_rows + offsets % sub_rows
    own_positions = (
        seq_index * tok_rows + fsdp_index * sub_rows + jnp.arange(sub_rows, dtype=jnp.int32)
    )

    def project(weight_block):
        return jnp.dot(hidden, weight_block, preferred_element_type=jnp.float32)

    query_part = project(lax.all_gather(w_query, "sp", axis=1, tiled=True))
    kv_part = project(lax.all_gather(w_keyvalue, "sp", axis=1, tiled=True))
    query_sum, kv_sum = (
        lax.psum_scatter(query_part, "fsdp", scatter_dimension=0, tiled=True),
        lax.psum_scatter(kv_part, "fsdp", scatter_dimension=0, tiled=True),
    )
    query_local = rotate(query_sum, own_positions, seq_count, HD).astype(jnp.bfloat16)
    pairs = split_keys(kv_sum, own_positions, kv_count, HD)
    expanded = jnp.repeat(pairs, GROUP, axis=1).reshape(sub_rows, seq_count * 2 * HD)
    query_head, kv_head = (
        lax.all_to_all(query_local, "sp", split_axis=1, concat_axis=0, tiled=True),
        lax.all_to_all(expanded, "sp", split_axis=1, concat_axis=0, tiled=True),
    )
    segment_all = lax.all_gather(segment_ids, "sp", axis=0, tiled=True)
    query_seg = segment_all[query_pos]
    initial = (
        jnp.full((query_rows,), NEG_FILL, jnp.float32),
        jnp.zeros((query_rows,), jnp.float32),
        jnp.zeros((query_rows, HD), jnp.float32),
    )
    block_keys = lax.all_gather(kv_head, "fsdp", axis=0, tiled=True)
    piece_rows = block_keys.shape[0]
    row_ids = jnp.arange(piece_rows, dtype=jnp.int32)
    source_id = row_ids // query_rows
    within = row_ids % query_rows
    key_pos = within // sub_rows * tok_rows + source_id * sub_rows + within % sub_rows
    key_seg = segment_all[key_pos]
    final_max, final_sum, final_weighted = merge_keys(
        initial, query_head, query_pos, query_seg, block_keys, key_pos, key_seg
    )
    attention = (final_weighted / final_sum[:, None]).astype(jnp.bfloat16)
    back_rows = lax.all_to_all(attention, "sp", split_axis=0, concat_axis=1, tiled=True)
    mixed_rows = lax.all_gather(back_rows, "fsdp", axis=0, tiled=True)
    result = jnp.dot(
        mixed_rows,
        lax.all_gather(w_output, "sp", axis=0, tiled=True),
        preferred_element_type=jnp.float32,
    )
    return result.astype(jnp.bfloat16)


def solution(mesh):
    in_specs = (P("sp", "fsdp"), P("fsdp", "sp"), P("fsdp", "sp"), P("sp", "fsdp"), P("sp"))
    out_specs = P("sp", "fsdp")
    return jax.shard_map(
        on_device, mesh=mesh, in_specs=in_specs, out_specs=out_specs, check_vma=False
    )
```

profile of v0, /device:TPU:0, one launch (start us, length us, event | category | flops | bytes accessed | tf_op | source)
XLA Modules:
  0.0 280.8 jit_solution(3011996384781910842)
XLA Ops:
  6.5 0.7 all-gather.8.cloned.1.call-update
  7.3 0.7 all-gather.6.cloned.1.call-update
  8.1 44.4 %all-gather.8.cloned.1.call-done = bf16[2048,256]{0,1:T(8,128)(2,1)} async-done(((bf16[2048,32]{0,1:T(8,128)(2,1)}), bf16[2048,256]{0,1:T(8,128)(2,1)}) %all-gather.8.cloned.1.call-update) | async-done | bytes 1048592 | tf_op jit(solution)/shard_map/all_gather | solution.py:86
  52.5 2.4 fusion.62
  54.9 0.0 reduce-scatter.3.cloned.1.call-start
  55.0 72.9 %all-gather.6.cloned.1.call-done = bf16[2048,1024]{1,0:T(8,128)(2,1)} async-done(((bf16[2048,128]{1,0:T(8,128)(2,1)}), bf16[2048,1024]{1,0:T(8,128)(2,1)}) %all-gather.6.cloned.1.call-update) | async-done | bytes 4194320 | tf_op jit(solution)/shard_map/all_gather | solution.py:85
  127.9 4.4 %fusion.61 = f32[256,1024]{1,0:T(8,128)} fusion(bf16[256,2048]{1,0:T(8,128)(2,1)S(1)} %copy-done, bf16[2048,1024]{1,0:T(8,128)(2,1)} %all-gather.6.cloned.1.call-done), kind=kOutput, calls=%fused_computation.109 | convolution fusion | flops 1073741824 | bytes 6291456 | tf_op jit(solution)/shard_map/dot_general | solution.py:83
  132.3 0.0 all-gather.10.cloned.1.call-start
  132.4 16.3 %reduce-scatter.5.cloned.1.call-done = f32[64,256]{1,0:T(8,128)} async-done(((f32[256,256]{1,0:T(8,128)}), f32[64,256]{1,0:T(8,128)}) %reduce-scatter.5.cloned.1.call-update) | async-done | bytes 65552 | tf_op jit(solution)/shard_map/reduce_scatter | solution.py:89
  148.7 0.9 reshape.398
  149.7 0.2 fusion.19
  149.9 0.1 copy_bitcast_fusion.1
  150.0 14.1 %all_to_all.51 = bf16[64,8,256]{2,0,1:T(8,128)(2,1)} all-to-all(bf16[64,8,256]{2,0,1:T(8,128)(2,1)S(1)} %broadcast_in_dim.10), channel_id=1, replica_groups=mesh['fsdp'=4,'sp'=8] {'sp'}, dimensions={1} | all-to-all | bytes 524288 | tf_op jit(solution)/shard_map/all_to_all | solution.py:96
  164.1 0.0 all-gather.12.cloned.1.call-start
  164.1 0.5 all-gather.12.cloned.1.call-update
  164.7 0.2 multiply_cosine_fusion.1
  164.9 11.0 %reduce-scatter.3.cloned.1.call-done = f32[64,1024]{1,0:T(8,128)} async-done(((f32[256,1024]{1,0:T(8,128)}), f32[64,1024]{1,0:T(8,128)}) %reduce-scatter.3.cloned.1.call-update) | async-done | bytes 262160 | tf_op jit(solution)/shard_map/reduce_scatter | solution.py:88
  175.9 1.0 copy.25
  176.9 0.1 fusion.60
  177.0 0.1 subtract_convert_fusion
  177.2 0.8 pad_maximum_fusion
  177.9 5.5 %all-to-all-start = ((bf16[64,8,128]{2,0,1:T(8,128)(2,1)}), bf16[64,8,128]{2,0,1:T(8,128)(2,1)S(1)}, u32[]{:S(2)}, u32[]{:S(2)}) async-start(bf16[64,8,128]{2,0,1:T(8,128)(2,1)} %pad_maximum_fusion), calls=%async_computation.1 | async-start | bytes 262144 | tf_op jit(solution)/shard_map/all_to_all | solution.py:95
  183.5 21.0 %all-gather = s32[8,1,256]{2,1,0:T(1,128)S(1)} all-gather(s32[1,1,256]{2,1,0:T(1,128)S(1)} %bitcast.48), channel_id=1, replica_groups=mesh['fsdp'=4,'sp'=8] {'sp'}, dimensions={0}, use_global_device_ids=true | all-gather | bytes 9216 | tf_op jit(solution)/shard_map/all_gather | solution.py:98
  204.5 3.1 %gather_fusion.1 = s32[512]{0:T(512)S(1)} fusion(s32[2048]{0:T(1024)S(1)} %bitcast.37, s32[1024]{0:T(1024)S(1)} %pad_clamp_fusion), kind=kCustom, calls=%fused_computation.1 | custom fusion | bytes 6144 | tf_op jit(solution)/shard_map/gather | solution.py:99
  207.6 11.8 %gather_fusion = s32[2048]{0:T(1024)S(1)} fusion(s32[2048]{0:T(1024)S(1)} %bitcast.38, s32[2048]{0:T(1024)S(1)} %broadcast_clamp_fusion), kind=kCustom, calls=%fused_computation | custom fusion | bytes 24576 | tf_op jit(solution)/shard_map/gather | solution.py:111
  219.5 2.4 fusion
  221.8 1.7 fusion.1
  223.5 1.3 fusion.8
  224.8 9.8 %all_to_all.52 = bf16[8,64,128]{2,1,0:T(8,128)(2,1)S(1)} all-to-all(bf16[8,64,128]{2,1,0:T(8,128)(2,1)S(1)} %bitcast.44), channel_id=1, replica_groups=mesh['fsdp'=4,'sp'=8] {'sp'}, dimensions={0} | all-to-all | bytes 262144 | tf_op jit(solution)/shard_map/all_to_all | solution.py:116
  234.7 6.5 %all_gather.22 = bf16[256,1024]{1,0:T(8,128)(2,1)S(1)} all-gather(bf16[64,1024]{1,0:T(8,128)(2,1)S(1)} %copy_bitcast_fusion), channel_id=1, replica_groups=mesh['fsdp'=4,'sp'=8] {'fsdp'}, dimensions={0}, use_global_device_ids=true | all-gather | bytes 655360 | tf_op jit(solution)/shard_map/all_gather | solution.py:117
  241.2 28.3 %all-gather.12.cloned.1.call-done = bf16[1024,2048]{1,0:T(8,128)(2,1)} async-done(((bf16[128,2048]{1,0:T(8,128)(2,1)}), bf16[1024,2048]{1,0:T(8,128)(2,1)}) %all-gather.12.cloned.1.call-update) | async-done | bytes 4194320 | tf_op jit(solution)/shard_map/all_gather | solution.py:120
  269.5 4.4 %convolution_convert_fusion = bf16[256,2048]{1,0:T(8,128)(2,1)} fusion(bf16[256,1024]{1,0:T(8,128)(2,1)S(1)} %all_gather.22, bf16[1024,2048]{1,0:T(8,128)(2,1)} %all-gather.12.cloned.1.call-done), kind=kOutput, calls=%fused_computation.6 | convolution fusion | flops 1074266112 | bytes 5767168 | tf_op jit(solution)/shard_map/dot_general | solution.py:118
  (29 shorter events, 0.4 us)
Async XLA Ops:
  6.5 46.0 %copy-start = (bf16[256,2048]{1,0:T(8,128)(2,1)S(1)}, bf16[256,2048]{1,0:T(8,128)(2,1)}, u32[]{:S(2)}) copy-start(bf16[256,2048]{1,0:T(8,128)(2,1)} %param.5) | copy-start | bytes 3145732
  6.5 46.0 %all-gather.8.cloned.1.call-start = ((), (), s32[]{:S(2)}) async-start(), calls=%async_computation.7 | async-start | bytes 1179648 | tf_op jit(solution)/shard_map/all_gather | solution.py:86
  7.3 120.7 %all-gather.6.cloned.1.call-start = ((), (), s32[]{:S(2)}) async-start(), calls=%async_computation.5 | async-start | bytes 4718592 | tf_op jit(solution)/shard_map/all_gather | solution.py:85
  8.0 140.7 %reduce-scatter.5.cloned.1.call-start = ((), (), s32[]{:S(2)}) async-start(), calls=%async_computation.8 | async-start | bytes 327680 | tf_op jit(solution)/shard_map/reduce_scatter | solution.py:89
  54.9 121.0 %reduce-scatter.3.cloned.1.call-start = ((), (), s32[]{:S(2)}) async-start(), calls=%async_computation.6 | async-start | bytes 1310720 | tf_op jit(solution)/shard_map/reduce_scatter | solution.py:88
  132.3 51.1 %copy-start.1 = (s32[256]{0:T(256)S(1)}, s32[256]{0:T(256)}, u32[]{:S(2)}) copy-start(s32[256]{0:T(256)} %param.9) | copy-start | bytes 3076
  132.3 87.1 %all-gather.10.cloned.1.call-start = ((), (), s32[]{:S(2)}) async-start(), calls=%async_computation.9 | async-start | bytes 1310720 | tf_op jit(solution)/shard_map/all_gather | solution.py:105
  164.1 105.4 %all-gather.12.cloned.1.call-start = ((), (), s32[]{:S(2)}) async-start(), calls=%async_computation.10 | async-start | bytes 4718592 | tf_op jit(solution)/shard_map/all_gather | solution.py:120
  177.9 41.5 %all-to-all-start = ((bf16[64,8,128]{2,0,1:T(8,128)(2,1)}), bf16[64,8,128]{2,0,1:T(8,128)(2,1)S(1)}, u32[]{:S(2)}, u32[]{:S(2)}) async-start(bf16[64,8,128]{2,0,1:T(8,128)(2,1)} %pad_maximum_fusion), calls=%async_computation.1 | async-start | bytes 262144 | tf_op jit(solution)/shard_map/all_to_all | solution.py:95
  219.5 4.1 %copy-start.2 = (bf16[2048,256]{1,0:T(8,128)(2,1)S(1)}, bf16[2048,256]{1,0:T(8,128)(2,1)}, u32[]{:S(2)}) copy-start(bf16[2048,256]{1,0:T(8,128)(2,1)} %all-gather.10.cloned.1.call-done) | copy-start | bytes 3145732
Sparse Core Ops, SparseCore 0:
  9.5 42.9 all-gather.7
  54.5 73.3 all-gather.5
  130.4 18.2 reduce-scatter.4
  151.1 24.8 reduce-scatter.2
  177.3 16.6 all-gather.9
  196.0 73.3 all-gather.11
where the time goes:
time: 281 us
  waiting for transfers between devices  175 us (62%)
  blocking collectives  51.4 us (18%)
  local copies, waits for them, and re-layouts  17 us (6%)
  matrix products  14.9 us (5%)
  between operations  13.7 us (5%)
  starting transfers between devices  5.72 us (2%)
  other arithmetic  3.14 us (1%)
    all_gather x1, waiting for transfers between devices, on_device(): query_part = project(lax.all_gather(w_query, 'sp', axis=1, tiled=True))  72.9 us
    all_gather x1, waiting for transfers between devices, on_device(): kv_part = project(lax.all_gather(w_keyvalue, 'sp', axis=1, tiled=True))  44.4 us
    all_gather x1, waiting for transfers between devices, on_device(): lax.all_gather(w_output, 'sp', axis=0, tiled=True)  28.3 us
    all_gather x1, blocking collectives, on_device(): segment_all = lax.all_gather(segment_ids, 'sp', axis=0, tiled=True)  21 us
    reduce_scatter x1, waiting for transfers between devices, on_device(): lax.psum_scatter(kv_part, 'fsdp', scatter_dimension=0, tiled=True)  16.3 us
    all_to_all x1, blocking collectives, on_device(): lax.all_to_all(expanded, 'sp', split_axis=1, concat_axis=0, tiled=True)  14.1 us
    gather x1, local copies, waits for them, and re-layouts, on_device(): key_seg = segment_all[key_pos]  11.8 us
    reduce_scatter x1, waiting for transfers between devices, on_device(): lax.psum_scatter(query_part, 'fsdp', scatter_dimension=0, tiled=True)  11 us
  transfers between devices with their start and end apart: 7, of which 5 were waited for; matrix products, arithmetic and copies ran while one was open for 11% of the time, Pallas kernels for 0%

commit v1 on v0

--- a/solution.py
+++ b/solution.py
@@ -95,7 +95,14 @@
         lax.all_to_all(query_local, "sp", split_axis=1, concat_axis=0, tiled=True),
         lax.all_to_all(expanded, "sp", split_axis=1, concat_axis=0, tiled=True),
     )
-    segment_all = lax.all_gather(segment_ids, "sp", axis=0, tiled=True)
+    size = lax.axis_size("sp")
+    forward = [(i, (i + 1) % size) for i in range(size)]
+    parts = [segment_ids]
+    for reach in range(1, size):
+        parts = [lax.ppermute(parts[0], "sp", forward), *parts]
+    result_2 = jnp.concatenate(parts, axis=0)
+    shift = (lax.axis_index("sp") + 1) * parts[-1].shape[0]
+    segment_all = jnp.roll(result_2, shift, axis=0)
     query_seg = segment_all[query_pos]
     initial = (
         jnp.full((query_rows,), NEG_FILL, jnp.float32),

time: 281 us -> 283 us (level)
  waiting for transfers between devices: 175 us -> 193 us
  blocking collectives: 51.4 us -> 35.9 us
    ppermute x0 -> x7, waiting for transfers between devices: none -> 42.3 us  [on_device(): parts = [lax.ppermute(parts[0], 'sp', forward), *parts]]
    all_gather x1 -> x0, blocking collectives: 21 us -> none  [on_device(): segment_all = lax.all_gather(segment_ids, 'sp', axis=0, tiled=True)]
    all_gather x1, waiting for transfers between devices: 28.3 us -> 15 us  [on_device(): lax.all_gather(w_output, 'sp', axis=0, tiled=True)]
    reduce_scatter x1, waiting for transfers between devices: 11 us -> 0.02 us  [on_device(): lax.psum_scatter(query_part, 'fsdp', scatter_dimension=0, tiled=True)]
    all_to_all x1, blocking collectives: 9.84 us -> 15 us  [on_device(): lax.all_to_all(attention, 'sp', split_axis=0, concat_axis=1, tiled=True)]
  transfers between devices with their start and end apart: 7 -> 14, of which waited for: 5 -> 11; matrix products, arithmetic and copies ran while one was open for 11% -> 11% of each run, Pallas kernels for 0% -> 0%
where the time goes in v1:
time: 283 us
  waiting for transfers between devices  193 us (68%)
  blocking collectives  35.9 us (13%)
  local copies, waits for them, and re-layouts  17.2 us (6%)
  matrix products  14.9 us (5%)
  between operations  13.8 us (5%)
  starting transfers between devices  5.06 us (2%)
  other arithmetic  3.14 us (1%)
    all_gather x1, waiting for transfers between devices, on_device(): query_part = project(lax.all_gather(w_query, 'sp', axis=1, tiled=True))  72.9 us
    all_gather x1, waiting for transfers between devices, on_device(): kv_part = project(lax.all_gather(w_keyvalue, 'sp', axis=1, tiled=True))  44.4 us
    ppermute x7, waiting for transfers between devices, on_device(): parts = [lax.ppermute(parts[0], 'sp', forward), *parts]  42.3 us
    reduce_scatter x1, waiting for transfers between devices, on_device(): lax.psum_scatter(kv_part, 'fsdp', scatter_dimension=0, tiled=True)  16.3 us
    all_gather x1, waiting for transfers between devices, on_device(): lax.all_gather(w_output, 'sp', axis=0, tiled=True)  15 us
    all_to_all x1, blocking collectives, on_device(): lax.all_to_all(attention, 'sp', split_axis=0, concat_axis=1, tiled=True)  15 us
    all_to_all x1, blocking collectives, on_device(): lax.all_to_all(expanded, 'sp', split_axis=1, concat_axis=0, tiled=True)  14.1 us
    gather x1, local copies, waits for them, and re-layouts, on_device(): key_seg = segment_all[key_pos]  11.8 us
  transfers between devices with their start and end apart: 14, of which 11 were waited for; matrix products, arithmetic and copies ran while one was open for 11% of the time, Pallas kernels for 0%

profile of v1, /device:TPU:0, one launch (start us, length us, event | category | flops | bytes accessed | tf_op | source)
XLA Modules:
  0.0 282.9 jit_solution(9061377041045727111)
XLA Ops:
  6.5 0.7 all-gather.7.cloned.1.call-update
  7.3 0.7 all-gather.5.cloned.1.call-update
  8.1 44.4 %all-gather.7.cloned.1.call-done = bf16[2048,256]{0,1:T(8,128)(2,1)} async-done(((bf16[2048,32]{0,1:T(8,128)(2,1)}), bf16[2048,256]{0,1:T(8,128)(2,1)}) %all-gather.7.cloned.1.call-update) | async-done | bytes 1048592 | tf_op jit(solution)/shard_map/all_gather | solution.py:86
  52.5 2.4 fusion.62
  55.0 72.9 %all-gather.5.cloned.1.call-done = bf16[2048,1024]{1,0:T(8,128)(2,1)} async-done(((bf16[2048,128]{1,0:T(8,128)(2,1)}), bf16[2048,1024]{1,0:T(8,128)(2,1)}) %all-gather.5.cloned.1.call-update) | async-done | bytes 4194320 | tf_op jit(solution)/shard_map/all_gather | solution.py:85
  127.9 4.4 %fusion.61 = f32[256,1024]{1,0:T(8,128)} fusion(bf16[256,2048]{1,0:T(8,128)(2,1)S(1)} %copy-done, bf16[2048,1024]{1,0:T(8,128)(2,1)} %all-gather.5.cloned.1.call-done), kind=kOutput, calls=%fused_computation.125 | convolution fusion | flops 1073741824 | bytes 6291456 | tf_op jit(solution)/shard_map/dot_general | solution.py:83
  132.4 16.3 %reduce-scatter.5.cloned.1.call-done = f32[64,256]{1,0:T(8,128)} async-done(((f32[256,256]{1,0:T(8,128)}), f32[64,256]{1,0:T(8,128)}) %reduce-scatter.5.cloned.1.call-update) | async-done | bytes 65552 | tf_op jit(solution)/shard_map/reduce_scatter | solution.py:89
  148.7 0.9 reshape.398
  149.7 0.2 fusion.19
  150.0 14.1 %all_to_all.51 = bf16[64,8,256]{2,0,1:T(8,128)(2,1)} all-to-all(bf16[64,8,256]{2,0,1:T(8,128)(2,1)S(1)} %broadcast_in_dim.10), channel_id=1, replica_groups=mesh['fsdp'=4,'sp'=8] {'sp'}, dimensions={1} | all-to-all | bytes 524288 | tf_op jit(solution)/shard_map/all_to_all | solution.py:96
  164.1 0.5 all-gather.11.cloned.1.call-update
  164.7 1.5 collective-permute-start
  166.1 0.2 multiply_cosine_fusion.1
  166.4 4.6 %collective-permute-done = s32[256]{0:T(256)S(1)} collective-permute-done((s32[256]{0:T(256)S(1)}, s32[256]{0:T(256)S(1)}, u32[]{:S(2)}, u32[]{:S(2)}) %collective-permute-start) | collective-permute-done | bytes 1056 | tf_op jit(solution)/shard_map/ppermute | solution.py:102
  171.0 6.3 %collective-permute-done.1 = s32[256]{0:T(256)S(1)} collective-permute-done((s32[256]{0:T(256)S(1)}, s32[256]{0:T(256)S(1)}, u32[]{:S(2)}, u32[]{:S(2)}) %collective-permute-start.1) | collective-permute-done | bytes 1056 | tf_op jit(solution)/shard_map/ppermute | solution.py:102
  177.3 6.3 %collective-permute-done.2 = s32[256]{0:T(256)S(1)} collective-permute-done((s32[256]{0:T(256)S(1)}, s32[256]{0:T(256)S(1)}, u32[]{:S(2)}, u32[]{:S(2)}) %collective-permute-start.2) | collective-permute-done | bytes 1056 | tf_op jit(solution)/shard_map/ppermute | solution.py:102
  183.6 6.3 %collective-permute-done.3 = s32[256]{0:T(256)S(1)} collective-permute-done((s32[256]{0:T(256)S(1)}, s32[256]{0:T(256)S(1)}, u32[]{:S(2)}, u32[]{:S(2)}) %collective-permute-start.3) | collective-permute-done | bytes 1056 | tf_op jit(solution)/shard_map/ppermute | solution.py:102
  189.8 6.3 %collective-permute-done.4 = s32[256]{0:T(256)S(1)} collective-permute-done((s32[256]{0:T(256)S(1)}, s32[256]{0:T(256)S(1)}, u32[]{:S(2)}, u32[]{:S(2)}) %collective-permute-start.4) | collective-permute-done | bytes 1056 | tf_op jit(solution)/shard_map/ppermute | solution.py:102
  196.1 6.3 %collective-permute-done.5 = s32[256]{0:T(256)S(1)} collective-permute-done((s32[256]{0:T(256)S(1)}, s32[256]{0:T(256)S(1)}, u32[]{:S(2)}, u32[]{:S(2)}) %collective-permute-start.5) | collective-permute-done | bytes 1056 | tf_op jit(solution)/shard_map/ppermute | solution.py:102
  202.4 6.4 %collective-permute-done.6 = s32[256]{0:T(256)S(1)} collective-permute-done((s32[256]{0:T(256)S(1)}, s32[256]{0:T(256)S(1)}, u32[]{:S(2)}, u32[]{:S(2)}) %collective-permute-start.6) | collective-permute-done | bytes 1056 | tf_op jit(solution)/shard_map/ppermute | solution.py:102
  208.9 1.0 copy.25
  210.2 0.8 pad_maximum_fusion
  210.9 3.4 %all-to-all-start = ((bf16[64,8,128]{2,0,1:T(8,128)(2,1)}), bf16[64,8,128]{2,0,1:T(8,128)(2,1)S(1)}, u32[]{:S(2)}, u32[]{:S(2)}) async-start(bf16[64,8,128]{2,0,1:T(8,128)(2,1)} %pad_maximum_fusion), calls=%async_computation.1 | async-start | bytes 262144 | tf_op jit(solution)/shard_map/all_to_all | solution.py:95
  214.5 11.8 %gather_fusion = s32[2048]{0:T(1024)S(1)} fusion(s32[2048]{0:T(1024)S(1)} %dynamic_slice.4, s32[2048]{0:T(1024)S(1)} %broadcast_clamp_fusion), kind=kCustom, calls=%fused_computation | custom fusion | bytes 24576 | tf_op jit(solution)/shard_map/gather | solution.py:118
  226.2 3.1 %gather_fusion.1 = s32[512]{0:T(512)S(1)} fusion(s32[2048]{0:T(1024)S(1)} %dynamic_slice.4, s32[1024]{0:T(1024)S(1)} %pad_clamp_fusion), kind=kCustom, calls=%fused_computation.1 | custom fusion | bytes 6144 | tf_op jit(solution)/shard_map/gather | solution.py:106
  229.4 2.4 fusion
  231.8 1.7 fusion.1
  233.5 1.3 fusion.8
  234.8 15.0 %all_to_all.52 = bf16[8,64,128]{2,1,0:T(8,128)(2,1)S(1)} all-to-all(bf16[8,64,128]{2,1,0:T(8,128)(2,1)S(1)} %bitcast.40), channel_id=1, replica_groups=mesh['fsdp'=4,'sp'=8] {'sp'}, dimensions={0} | all-to-all | bytes 262144 | tf_op jit(solution)/shard_map/all_to_all | solution.py:123
  249.8 6.8 %all_gather.18 = bf16[256,1024]{1,0:T(8,128)(2,1)S(1)} all-gather(bf16[64,1024]{1,0:T(8,128)(2,1)S(1)} %copy_bitcast_fusion), channel_id=1, replica_groups=mesh['fsdp'=4,'sp'=8] {'fsdp'}, dimensions={0}, use_global_device_ids=true | all-gather | bytes 655360 | tf_op jit(solution)/shard_map/all_gather | solution.py:124
  256.6 15.0 %all-gather.11.cloned.1.call-done = bf16[1024,2048]{1,0:T(8,128)(2,1)} async-done(((bf16[128,2048]{1,0:T(8,128)(2,1)}), bf16[1024,2048]{1,0:T(8,128)(2,1)}) %all-gather.11.cloned.1.call-update) | async-done | bytes 4194320 | tf_op jit(solution)/shard_map/all_gather | solution.py:127
  271.6 4.4 %convolution_convert_fusion = bf16[256,2048]{1,0:T(8,128)(2,1)} fusion(bf16[256,1024]{1,0:T(8,128)(2,1)S(1)} %all_gather.18, bf16[1024,2048]{1,0:T(8,128)(2,1)} %all-gather.11.cloned.1.call-done), kind=kOutput, calls=%fused_computation.6 | convolution fusion | flops 1074266112 | bytes 5767168 | tf_op jit(solution)/shard_map/dot_general | solution.py:125
  (60 shorter events, 1.0 us)
Async XLA Ops:
  6.5 46.0 %copy-start = (bf16[256,2048]{1,0:T(8,128)(2,1)S(1)}, bf16[256,2048]{1,0:T(8,128)(2,1)}, u32[]{:S(2)}) copy-start(bf16[256,2048]{1,0:T(8,128)(2,1)} %param.5) | copy-start | bytes 3145732
  6.5 46.0 %all-gather.7.cloned.1.call-start = ((), (), s32[]{:S(2)}) async-start(), calls=%async_computation.7 | async-start | bytes 1179648 | tf_op jit(solution)/shard_map/all_gather | solution.py:86
  7.3 120.7 %all-gather.5.cloned.1.call-start = ((), (), s32[]{:S(2)}) async-start(), calls=%async_computation.5 | async-start | bytes 4718592 | tf_op jit(solution)/shard_map/all_gather | solution.py:85
  8.0 140.7 %reduce-scatter.5.cloned.1.call-start = ((), (), s32[]{:S(2)}) async-start(), calls=%async_computation.8 | async-start | bytes 327680 | tf_op jit(solution)/shard_map/reduce_scatter | solution.py:89
  54.9 109.8 %copy-start.1 = (s32[256]{0:T(256)S(1)}, s32[256]{0:T(256)}, u32[]{:S(2)}) copy-start(s32[256]{0:T(256)} %param.9) | copy-start | bytes 3076
  54.9 154.0 %reduce-scatter.3.cloned.1.call-start = ((), (), s32[]{:S(2)}) async-start(), calls=%async_computation.6 | async-start | bytes 1310720 | tf_op jit(solution)/shard_map/reduce_scatter | solution.py:88
  132.3 97.1 %all-gather.9.cloned.1.call-start = ((), (), s32[]{:S(2)}) async-start(), calls=%async_computation.9 | async-start | bytes 1310720 | tf_op jit(solution)/shard_map/all_gather | solution.py:112
  164.1 107.5 %all-gather.11.cloned.1.call-start = ((), (), s32[]{:S(2)}) async-start(), calls=%async_computation.10 | async-start | bytes 4718592 | tf_op jit(solution)/shard_map/all_gather | solution.py:127
  164.7 6.3 %collective-permute-start = (s32[256]{0:T(256)S(1)}, s32[256]{0:T(256)S(1)}, u32[]{:S(2)}, u32[]{:S(2)}) collective-permute-start(s32[256]{0:T(256)S(1)} %copy-done.1), channel_id=1, source_target_pairs={{0,1},{1,2},{2,3},{3,4},{4,5},{5,6},{6,7},{7,0},{8,9},{9,10},{10,1... | collective-permute-start | bytes 3080 | tf_op jit(solution)/shard_map/ppermute | solution.py:102
  171.0 6.3 %collective-permute-start.1 = (s32[256]{0:T(256)S(1)}, s32[256]{0:T(256)S(1)}, u32[]{:S(2)}, u32[]{:S(2)}) collective-permute-start(s32[256]{0:T(256)S(1)} %collective-permute-done), channel_id=1, source_target_pairs={{0,1},{1,2},{2,3},{3,4},{4,5},{5,6},{6,7},{7,0},{8,9},{9,10},{10,1... | collective-permute-start | bytes 3080 | tf_op jit(solution)/shard_map/ppermute | solution.py:102
  177.3 6.3 %collective-permute-start.2 = (s32[256]{0:T(256)S(1)}, s32[256]{0:T(256)S(1)}, u32[]{:S(2)}, u32[]{:S(2)}) collective-permute-start(s32[256]{0:T(256)S(1)} %collective-permute-done.1), channel_id=1, source_target_pairs={{0,1},{1,2},{2,3},{3,4},{4,5},{5,6},{6,7},{7,0},{8,9},{9,10},{10,1... | collective-permute-start | bytes 3080 | tf_op jit(solution)/shard_map/ppermute | solution.py:102
  183.5 6.3 %collective-permute-start.3 = (s32[256]{0:T(256)S(1)}, s32[256]{0:T(256)S(1)}, u32[]{:S(2)}, u32[]{:S(2)}) collective-permute-start(s32[256]{0:T(256)S(1)} %collective-permute-done.2), channel_id=1, source_target_pairs={{0,1},{1,2},{2,3},{3,4},{4,5},{5,6},{6,7},{7,0},{8,9},{9,10},{10,1... | collective-permute-start | bytes 3080 | tf_op jit(solution)/shard_map/ppermute | solution.py:102
  189.8 6.3 %collective-permute-start.4 = (s32[256]{0:T(256)S(1)}, s32[256]{0:T(256)S(1)}, u32[]{:S(2)}, u32[]{:S(2)}) collective-permute-start(s32[256]{0:T(256)S(1)} %collective-permute-done.3), channel_id=1, source_target_pairs={{0,1},{1,2},{2,3},{3,4},{4,5},{5,6},{6,7},{7,0},{8,9},{9,10},{10,1... | collective-permute-start | bytes 3080 | tf_op jit(solution)/shard_map/ppermute | solution.py:102
  196.1 6.3 %collective-permute-start.5 = (s32[256]{0:T(256)S(1)}, s32[256]{0:T(256)S(1)}, u32[]{:S(2)}, u32[]{:S(2)}) collective-permute-start(s32[256]{0:T(256)S(1)} %collective-permute-done.4), channel_id=1, source_target_pairs={{0,1},{1,2},{2,3},{3,4},{4,5},{5,6},{6,7},{7,0},{8,9},{9,10},{10,1... | collective-permute-start | bytes 3080 | tf_op jit(solution)/shard_map/ppermute | solution.py:102
  202.4 6.4 %collective-permute-start.6 = (s32[256]{0:T(256)S(1)}, s32[256]{0:T(256)S(1)}, u32[]{:S(2)}, u32[]{:S(2)}) collective-permute-start(s32[256]{0:T(256)S(1)} %collective-permute-done.5), channel_id=1, source_target_pairs={{0,1},{1,2},{2,3},{3,4},{4,5},{5,6},{6,7},{7,0},{8,9},{9,10},{10,1... | collective-permute-start | bytes 3080 | tf_op jit(solution)/shard_map/ppermute | solution.py:102
  210.9 18.5 %all-to-all-start = ((bf16[64,8,128]{2,0,1:T(8,128)(2,1)}), bf16[64,8,128]{2,0,1:T(8,128)(2,1)S(1)}, u32[]{:S(2)}, u32[]{:S(2)}) async-start(bf16[64,8,128]{2,0,1:T(8,128)(2,1)} %pad_maximum_fusion), calls=%async_computation.1 | async-start | bytes 262144 | tf_op jit(solution)/shard_map/all_to_all | solution.py:95
  229.4 4.1 %copy-start.2 = (bf16[2048,256]{1,0:T(8,128)(2,1)S(1)}, bf16[2048,256]{1,0:T(8,128)(2,1)}, u32[]{:S(2)}) copy-start(bf16[2048,256]{1,0:T(8,128)(2,1)} %all-gather.9.cloned.1.call-done) | copy-start | bytes 3145732
Sparse Core Ops, SparseCore 0:
  9.5 42.9 all-gather.6
  54.5 73.3 all-gather.4
  130.4 18.2 reduce-scatter.4
  151.1 24.8 reduce-scatter.2
  177.3 16.7 all-gather.8
  196.1 75.4 all-gather.10
